TPU v7x, 32 devices: a whole 2x2x4 slice. The times are simulated.
32 devices in a mesh: dp: 4 (over y, core), ctx: 8 (over z, x).
Axes of the slice: x: 2, y: 2, z: 4, core: 2. Of those that a mesh axis runs over, the one named last changes fastest.
Arguments:
- text: bfloat16 [4, 2, 128, 2048], P('dp', None, None, 'ctx'), may hold values from -6 to 6
- src: int32 [4], replicated, may hold values from 0 to 3, each once
- lengths: int32 [4, 2], replicated, may hold values from 1 to 128
- kv_weight: bfloat16 [2048, 2, 8192], P('dp', None, 'ctx'), may hold values from -0.125 to 0.125
- queries: bfloat16 [4, 2048, 4096], P('dp', 'ctx'), may hold values from -160 to 160
- grad_out: bfloat16 [4, 2048, 4096], P('dp', 'ctx'), may hold values from -6 to 6
Outputs:
- attended: bfloat16 [4, 2048, 4096], P('dp', 'ctx')
- grad_queries: bfloat16 [4, 2048, 4096], P('dp', 'ctx')
- grad_weight: float32 [2048, 2, 8192], P('dp', None, 'ctx')
Inputs may be any that keep to these rules, and one draw needn't show every extreme that they name: `src`: each text sample is used by exactly one latent sample. `lengths`: tokens of an encoder output at or beyond its length are padding.
All inputs are finite; a program needn't handle non-finite values.
Results may differ from a plain program's by a relative error of at most 0.018.
The roundings to bfloat16 on the way count: a program that leaves them out, or rounds other values in their place, can miss the bound.
Values may be sent and summed in bfloat16 or wider, within the bound.
A program may use at most 128 MiB of HBM per device.

v0:
```python
import math

import jax
import jax.numpy as jnp
from jax import lax
from jax.sharding import PartitionSpec as P

HEAD = 128


def attend(queries, key_value, valid, grad_out):
    batch, length, width = queries.shape
    heads = width // HEAD
    keys = key_value.shape[1] * key_value.shape[2]
    scale = 1.0 / math.sqrt(HEAD)
    paired = key_value.reshape(batch, keys, heads, 2, HEAD)
    key = paired[:, :, :, 0]
    value = paired[:, :, :, 1]
    q_rows = queries.reshape(batch, length, heads, HEAD)
    g_rows = grad_out.reshape(batch, length, heads, HEAD)
    scores = jnp.einsum("blhd,bjhd->bhlj", q_rows, key, preferred_element_type=jnp.float32) * scale
    scores = jnp.where(valid[:, None, None, :], scores, -1e30)
    top = jnp.max(scores, axis=-1, keepdims=True)
    weights = jnp.exp(scores - top)
    probs = weights / jnp.sum(weights, axis=-1, keepdims=True)
    probs_low = probs.astype(jnp.bfloat16)
    attended = jnp.einsum("bhlj,bjhd->blhd", probs_low, value, preferred_element_type=jnp.float32)
    attended = attended.reshape(batch, length, width).astype(jnp.bfloat16)
    grad_probs = jnp.einsum("blhd,bjhd->bhlj", g_rows, value, preferred_element_type=jnp.float32)
    delta = jnp.sum(probs * grad_probs, axis=-1, keepdims=True)
    grad_scores = (probs * (grad_probs - delta) * scale).astype(jnp.bfloat16)
    grad_queries = jnp.einsum(
        "bhlj,bjhd->blhd", grad_scores, key, preferred_element_type=jnp.float32
    )
    grad_queries = grad_queries.reshape(batch, length, width).astype(jnp.bfloat16)
    grad_key = jnp.einsum(
        "bhlj,blhd->bjhd", grad_scores, q_rows, preferred_element_type=jnp.float32
    )
    grad_value = jnp.einsum(
        "bhlj,blhd->bjhd", probs_low, g_rows, preferred_element_type=jnp.float32
    )
    grad_kv = jnp.stack([grad_key, grad_value], axis=3).reshape(
        batch, 2, keys // 2, heads * 2 * HEAD
    )
    return (attended, grad_queries, grad_kv)


def per_device(text, src, lengths, kv_weight, queries, grad_out):
    per_group = queries.shape[0]
    group = lax.axis_index("dp")
    everyone = lax.all_gather(text, "dp", axis=0, tiled=True)
    chosen_ids = lax.dynamic_slice_in_dim(src, group * per_group, per_group, 0)
    picked = jnp.take(everyone, chosen_ids, axis=0)
    full_text = lax.all_gather(picked, "ctx", axis=3, tiled=True)
    tokens = full_text.shape[2]
    rows = full_text
    kv_local = jnp.einsum(
        "betf,fec->betc",
        rows,
        lax.all_gather(kv_weight, "dp", axis=0, tiled=True),
        preferred_element_type=jnp.float32,
    ).astype(jnp.bfloat16)
    chosen_lengths = jnp.take(lengths, chosen_ids, axis=0)
    positions = jnp.arange(tokens, dtype=jnp.int32)
    valid = (positions[None, None, :] < chosen_lengths[:, :, None]).reshape(per_group, 2 * tokens)
    moved_queries, moved_grads = (
        lax.all_to_all(queries, "ctx", split_axis=2, concat_axis=1, tiled=True),
        lax.all_to_all(grad_out, "ctx", split_axis=2, concat_axis=1, tiled=True),
    )
    head_out, head_grad, grad_kv = attend(moved_queries, kv_local, valid, moved_grads)
    attended, grad_queries = (
        lax.all_to_all(head_out, "ctx", split_axis=1, concat_axis=2, tiled=True),
        lax.all_to_all(head_grad, "ctx", split_axis=1, concat_axis=2, tiled=True),
    )
    grad_low = grad_kv.astype(jnp.bfloat16)
    rows = full_text
    grad_weight = lax.psum_scatter(
        jnp.einsum("betf,betc->fec", rows, grad_low, preferred_element_type=jnp.float32).astype(
            jnp.bfloat16
        ),
        "dp",
        scatter_dimension=0,
        tiled=True,
    ).astype(jnp.float32)
    return (attended, grad_queries, grad_weight)


def solution(mesh):
    placed = (
        P("dp", None, None, "ctx"),
        P(),
        P(),
        P("dp", None, "ctx"),
        P("dp", "ctx", None),
        P("dp", "ctx", None),
    )
    return jax.shard_map(
        per_device,
        mesh=mesh,
        in_specs=placed,
        out_specs=(P("dp", "ctx", None), P("dp", "ctx", None), P("dp", None, "ctx")),
        check_vma=False,
    )
```

profile of v0, /device:TPU:0, one launch (start us, length us, event | category | flops | bytes accessed | tf_op | source)
XLA Modules:
  0.0 400.6 jit_solution(18149222278047048982)
XLA Ops:
  7.2 1.4 dynamic_slice.3
  10.6 8.9 %all_gather.9 = bf16[4,2,128,256]{3,2,1,0:T(8,128)(2,1)S(1)} all-gather(bf16[1,2,128,256]{3,2,1,0:T(8,128)(2,1)} %param.6), channel_id=1, replica_groups=mesh['dp'=4,'ctx'=8] {'dp'}, dimensions={0}, use_global_device_ids=true | all-gather | bytes 655360 | tf_op jit(solution)/shard_map/all_gather | solution.py:51
  20.2 3.5 copy.79
  23.7 7.1 %copy.82 = bf16[1,256,4096]{1,0,2:T(2,128)(2,1)} copy(bf16[1,256,4096]{2,1,0:T(8,128)(2,1)S(1)} %copy-done.1) | data formatting | bytes 4194304 | tf_op args[4]
  31.3 21.5 %reduce.8 = bf16[4096,256]{1,0:T(8,128)(2,1)S(1)} reduce(bf16[4096,1,256]{2,1,0:T(2,128)(2,1)} %bitcast.142, bf16[]{:T(256)} %broadcast.122), dimensions={1}, to_apply=%bitcast.123.reduce_sub_computation | reduce | bytes 4194306
  52.8 3.2 reshape.226
  56.0 5.8 %all-to-all-start = ((bf16[8,2,65536]{2,1,0:T(2,128)(2,1)}), bf16[8,2,65536]{2,1,0:T(2,128)(2,1)S(1)}, u32[]{:S(2)}, u32[]{:S(2)}) async-start(bf16[8,2,65536]{2,1,0:T(2,128)(2,1)} %reshape.226), calls=%async_computation | async-start | bytes 4194304 | tf_op jit(solution)/shard_map/all_to_all | solution.py:67
  61.8 10.1 %copy.88 = bf16[1,256,4096]{1,0,2:T(2,128)(2,1)} copy(bf16[1,256,4096]{2,1,0:T(8,128)(2,1)} %param.11) | data formatting | bytes 4194304 | tf_op args[5]
  71.9 22.8 %reduce.10 = bf16[4096,256]{1,0:T(8,128)(2,1)} reduce(bf16[4096,1,256]{2,1,0:T(2,128)(2,1)} %bitcast.149, bf16[]{:T(256)} %broadcast.122), dimensions={1}, to_apply=%bitcast.121.reduce_sub_computation | reduce | bytes 4194306
  94.7 5.8 %reshape.224 = bf16[8,2,65536]{2,1,0:T(2,128)(2,1)} reshape(bf16[4096,256]{1,0:T(8,128)(2,1)} %reduce.10) | data formatting | bytes 4194304
  100.6 10.0 %all-to-all-done = bf16[8,2,65536]{2,1,0:T(2,128)(2,1)S(1)} async-done(((bf16[8,2,65536]{2,1,0:T(2,128)(2,1)}), bf16[8,2,65536]{2,1,0:T(2,128)(2,1)S(1)}, u32[]{:S(2)}, u32[]{:S(2)}) %all-to-all-start) | async-done | bytes 2097184 | tf_op jit(solution)/shard_map/all_to_all | solution.py:67
  110.5 4.4 %all-to-all-start.2 = ((bf16[8,2,65536]{2,1,0:T(2,128)(2,1)}), bf16[8,2,65536]{2,1,0:T(2,128)(2,1)}, u32[]{:S(2)}, u32[]{:S(2)}) async-start(bf16[8,2,65536]{2,1,0:T(2,128)(2,1)} %reshape.224), calls=%async_computation.2 | async-start | bytes 4194304 | tf_op jit(solution)/shard_map/all_to_all | solution.py:68
  115.5 4.3 %reshape.227 = bf16[4096,1,256]{2,1,0:T(2,128)(2,1)} reshape(bf16[8,2,65536]{2,1,0:T(2,128)(2,1)S(1)} %all-to-all-done) | data formatting | bytes 4194304
  119.8 2.5 copy.112
  123.6 2.3 reshape.172
  125.9 36.9 %all-to-all-done.2 = bf16[8,2,65536]{2,1,0:T(2,128)(2,1)} async-done(((bf16[8,2,65536]{2,1,0:T(2,128)(2,1)}), bf16[8,2,65536]{2,1,0:T(2,128)(2,1)}, u32[]{:S(2)}, u32[]{:S(2)}) %all-to-all-start.2) | async-done | bytes 2097184 | tf_op jit(solution)/shard_map/all_to_all | solution.py:68
  162.8 6.7 %reshape.225 = bf16[4096,1,256]{2,1,0:T(2,128)(2,1)} reshape(bf16[8,2,65536]{2,1,0:T(2,128)(2,1)} %all-to-all-done.2) | data formatting | bytes 4194304
  169.5 2.5 copy.114
  172.1 2.5 copy.89
  174.6 2.9 reshape.173
  177.5 5.0 %fusion.19 = bf16[1,2,128,1024]{3,2,1,0:T(8,128)(2,1)S(1)} fusion(bf16[2048,2,1024]{2,0,1:T(8,128)(2,1)} %all-gather.5.cloned.1.call-done, bf16[1,2,128,2048]{3,2,1,0:T(8,128)(2,1)} %all-gather.3.cloned.1.call-done), kind=kOutput, calls=%fused_computation.26 | convolution fusion | flops 1074003968 | bytes 9961472 | tf_op jit(solution)/shard_map/betf,fec->betc/dot_general | solution.py:57
  182.9 1.5 fusion.42
  185.4 4.5 %fusion.32 = f32[4,256,2048]{2,1,0:T(8,128)} fusion(bf16[2048,4,128]{0,2,1:T(8,128)(2,1)S(1)} %reshape.173, bf16[1,256,4,1,128]{1,4,2,3,0:T(8,128)(2,1)S(1)} %copy.116), kind=kOutput, calls=%fused_computation.36 | convolution fusion | flops 536870912 | bytes 10747904 | tf_op jit(solution)/shard_map/blhd,bjhd->bhlj/dot_general | solution.py:29
  189.9 8.0 %fusion.43 = (f32[4,2048]{1,0:T(4,128)S(1)}, f32[4,2048,256]{1,2,0:T(8,128)}) fusion(pred[256]{0:T(512)(128)(4,1)S(1)} %bitcast_compare_fusion, bf16[2048,4,128]{0,2,1:T(8,128)(2,1)} %reshape.172, bf16[1,256,4,1,128]{4,3,2,1,0:T(2,128)(2,1)S(1)} %copy-done.2), kind=kOutput, calls=%fused_computation.50 | convolution fusion | flops 545259776 | bytes 10780928 | tf_op jit(solution)/shard_map/sub | solution.py:24
  197.9 4.6 %fusion.24 = bf16[1,256,4,1,128]{4,1,2,3,0:T(8,128)(2,1)S(1)} fusion(bf16[2048,4,128]{0,2,1:T(8,128)(2,1)S(1)} %reshape.173, f32[4,2048,256]{1,2,0:T(8,128)} %get-tuple-element.43, f32[4,2048]{1,0:T(4,128)S(1)} %get-tuple-element.42), kind=kOutput, calls=%fused_computation.29 | convolution fusion | flops 541196288 | bytes 10780672 | tf_op jit(solution)/shard_map/bhlj,blhd->bjhd/dot_general | solution.py:39
  202.6 14.9 %fusion.27 = bf16[1,256,4,1,128]{4,1,2,3,0:T(8,128)(2,1)S(1)} fusion(bf16[2048,4,128]{0,2,1:T(8,128)(2,1)} %reshape.172, f32[4,256,2048]{2,1,0:T(8,128)} %fusion.32, f32[4,2048,256]{1,2,0:T(8,128)} %get-tuple-element.43, f32[4,2048]{1,0:T(4,128)S(1)} %get-tuple-element.42), kind=kOutput, calls=%fused_computation.30 | convolution fusion | flops 551690496 | bytes 19169280 | tf_op jit(solution)/shard_map/bhlj,blhd->bjhd/dot_general | solution.py:36
  218.4 5.6 %convert_bitcast_fusion = bf16[2048,2,1024]{0,2,1:T(8,128)(2,1)} fusion(bf16[2,128,1024]{2,1,0:T(8,128)(2,1)S(1)} %convert_element_type.90, bf16[1,2,128,2048]{3,2,1,0:T(8,128)(2,1)S(1)} %copy-done), kind=kOutput, calls=%fused_computation.11 | convolution fusion | flops 1077936128 | bytes 9961472 | tf_op jit(solution)/shard_map/betf,betc->fec/dot_general | solution.py:78
  224.0 18.2 %fusion.15 = bf16[4,128,2048]{2,1,0:T(8,128)(2,1)S(1)} fusion(f32[4,256,2048]{2,1,0:T(8,128)} %fusion.32, bf16[1,256,4,1,128]{4,3,2,1,0:T(2,128)(2,1)S(1)} %copy-done.2, f32[4,2048,256]{1,2,0:T(8,128)} %get-tuple-element.43, f32[4,2048]{1,0:T(4,128)S(1)} %get-tuple-element.42), kind=kOutput, calls=%fused_computation.20 | convolution fusion | flops 552608000 | bytes 19169280 | tf_op jit(solution)/shard_map/bhlj,bjhd->blhd/dot_general | solution.py:32
  242.3 7.5 %copy.94 = bf16[1,2048,512]{2,0,1:T(2,128)(2,1)} copy(bf16[1,2048,512]{1,2,0:T(8,128)(2,1)S(1)} %bitcast.157) | data formatting | bytes 4194304 | tf_op jit(solution)/shard_map/convert_element_type | solution.py:35
  249.8 14.0 %reduce.11 = bf16[2048,512]{1,0:T(8,128)(2,1)S(1)} reduce(bf16[2048,1,512]{2,1,0:T(2,128)(2,1)} %bitcast.146, bf16[]{:T(256)} %broadcast.122), dimensions={1}, to_apply=%bitcast.127.reduce_sub_computation | reduce | bytes 4194306
  263.8 3.8 reshape.230
  267.6 3.6 all-to-all-start.3
  271.2 5.7 %convolution_convert_fusion = bf16[4,128,2048]{2,1,0:T(8,128)(2,1)} fusion(bf16[1,256,4,1,128]{1,4,2,3,0:T(8,128)(2,1)S(1)} %copy.116, f32[4,2048,256]{1,2,0:T(8,128)} %get-tuple-element.43, f32[4,2048]{1,0:T(4,128)S(1)} %get-tuple-element.42), kind=kOutput, calls=%fused_computation.21 | convolution fusion | flops 542113792 | bytes 10780672 | tf_op jit(solution)/shard_map/bhlj,bjhd->blhd/dot_general | solution.py:27
  276.9 10.8 %copy.86 = bf16[1,2048,512]{2,0,1:T(2,128)(2,1)} copy(bf16[1,2048,512]{1,2,0:T(8,128)(2,1)} %bitcast.156) | data formatting | bytes 4194304 | tf_op jit(solution)/shard_map/convert_element_type | solution.py:28
  287.6 15.3 %reduce.9 = bf16[2048,512]{1,0:T(8,128)(2,1)} reduce(bf16[2048,1,512]{2,1,0:T(2,128)(2,1)} %bitcast.143, bf16[]{:T(256)} %broadcast.122), dimensions={1}, to_apply=%bitcast.125.reduce_sub_computation | reduce | bytes 4194306
  302.9 6.3 %reshape.228 = bf16[8,2,65536]{2,1,0:T(2,128)(2,1)} reshape(bf16[2048,512]{1,0:T(8,128)(2,1)} %reduce.9) | data formatting | bytes 4194304
  309.2 9.8 %all-to-all-done.3 = bf16[8,2,65536]{2,1,0:T(2,128)(2,1)S(1)} async-done(((bf16[8,2,65536]{2,1,0:T(2,128)(2,1)}), bf16[8,2,65536]{2,1,0:T(2,128)(2,1)S(1)}, u32[]{:S(2)}, u32[]{:S(2)}) %all-to-all-start.3) | async-done | bytes 2097184 | tf_op jit(solution)/shard_map/all_to_all | solution.py:73
  319.1 4.6 %all-to-all-start.1 = ((bf16[8,2,65536]{2,1,0:T(2,128)(2,1)}), bf16[8,2,65536]{2,1,0:T(2,128)(2,1)}, u32[]{:S(2)}, u32[]{:S(2)}) async-start(bf16[8,2,65536]{2,1,0:T(2,128)(2,1)} %reshape.228), calls=%async_computation.1 | async-start | bytes 4194304 | tf_op jit(solution)/shard_map/all_to_all | solution.py:72
  323.6 4.3 %reshape.231 = bf16[2048,1,512]{2,1,0:T(2,128)(2,1)} reshape(bf16[8,2,65536]{2,1,0:T(2,128)(2,1)S(1)} %all-to-all-done.3) | data formatting | bytes 4194304
  328.0 2.8 copy.115
  330.8 2.4 copy.95
  333.1 4.1 %copy.101 = bf16[1,256,4096]{2,1,0:T(8,128)(2,1)} copy(bf16[1,256,4096]{1,2,0:T(8,128)(2,1)} %bitcast.154) | data formatting | bytes 4194304
  337.2 34.2 %all-to-all-done.1 = bf16[8,2,65536]{2,1,0:T(2,128)(2,1)} async-done(((bf16[8,2,65536]{2,1,0:T(2,128)(2,1)}), bf16[8,2,65536]{2,1,0:T(2,128)(2,1)}, u32[]{:S(2)}, u32[]{:S(2)}) %all-to-all-start.1) | async-done | bytes 2097184 | tf_op jit(solution)/shard_map/all_to_all | solution.py:72
  371.4 6.7 %reshape.229 = bf16[2048,1,512]{2,1,0:T(2,128)(2,1)} reshape(bf16[8,2,65536]{2,1,0:T(2,128)(2,1)} %all-to-all-done.1) | data formatting | bytes 4194304
  378.2 2.8 copy.113
  381.0 2.4 copy.87
  383.3 4.1 %copy.100 = bf16[1,256,4096]{2,1,0:T(8,128)(2,1)} copy(bf16[1,256,4096]{1,2,0:T(8,128)(2,1)} %bitcast.155) | data formatting | bytes 4194304
  387.4 6.5 %copy.102 = f32[512,2,1024]{2,1,0:T(2,128)} copy(bf16[512,2,1024]{0,2,1:T(8,128)(2,1)} %reduce-scatter.2.cloned.1.call-done) | data formatting | bytes 6291456
  (28 shorter events, 5.4 us)
Async XLA Ops:
  7.2 16.6 %copy-start.1 = (bf16[1,256,4096]{2,1,0:T(8,128)(2,1)S(1)}, bf16[1,256,4096]{2,1,0:T(8,128)(2,1)}, u32[]{:S(2)}) copy-start(bf16[1,256,4096]{2,1,0:T(8,128)(2,1)} %param.10) | copy-start | bytes 6291460
  7.2 170.3 %all-gather.3.cloned.1.call-start = ((), (), s32[]{:S(2)}) async-start(), calls=%async_computation.5 | async-start | bytes 1179648 | tf_op jit(solution)/shard_map/all_gather | solution.py:54
  20.1 157.4 %all-gather.5.cloned.1.call-start = ((), (), s32[]{:S(2)}) async-start(), calls=%async_computation.6 | async-start | bytes 10485760 | tf_op jit(solution)/shard_map/all_gather | solution.py:60
  56.0 54.6 %all-to-all-start = ((bf16[8,2,65536]{2,1,0:T(2,128)(2,1)}), bf16[8,2,65536]{2,1,0:T(2,128)(2,1)S(1)}, u32[]{:S(2)}, u32[]{:S(2)}) async-start(bf16[8,2,65536]{2,1,0:T(2,128)(2,1)} %reshape.226), calls=%async_computation | async-start | bytes 4194304 | tf_op jit(solution)/shard_map/all_to_all | solution.py:67
  94.7 20.5 %copy-start.3 = (s32[4,2]{0,1:T(2,128)S(1)}, s32[4,2]{0,1:T(2,128)}, u32[]{:S(2)}) copy-start(s32[4,2]{0,1:T(2,128)} %param.8) | copy-start | bytes 100
  110.5 52.3 %all-to-all-start.2 = ((bf16[8,2,65536]{2,1,0:T(2,128)(2,1)}), bf16[8,2,65536]{2,1,0:T(2,128)(2,1)}, u32[]{:S(2)}, u32[]{:S(2)}) async-start(bf16[8,2,65536]{2,1,0:T(2,128)(2,1)} %reshape.224), calls=%async_computation.2 | async-start | bytes 4194304 | tf_op jit(solution)/shard_map/all_to_all | solution.py:68
  114.9 272.5 %reduce-scatter.2.cloned.1.call-start = ((), (), s32[]{:S(2)}) async-start(), calls=%async_computation.7 | async-start | bytes 10485760 | tf_op jit(solution)/shard_map/reduce_scatter | solution.py:77
  185.4 4.5 %copy-start.2 = (bf16[1,256,4,1,128]{4,3,2,1,0:T(2,128)(2,1)S(1)}, bf16[1,256,4,1,128]{4,3,2,1,0:T(2,128)(2,1)}, u32[]{:S(2)}) copy-start(bf16[1,256,4,1,128]{4,3,2,1,0:T(2,128)(2,1)} %get-tuple-element.40) | copy-start | bytes 786436
  202.5 15.9 %copy-start = (bf16[1,2,128,2048]{3,2,1,0:T(8,128)(2,1)S(1)}, bf16[1,2,128,2048]{3,2,1,0:T(8,128)(2,1)}, u32[]{:S(2)}) copy-start(bf16[1,2,128,2048]{3,2,1,0:T(8,128)(2,1)} %all-gather.3.cloned.1.call-done) | copy-start | bytes 3145732
  267.6 51.5 %all-to-all-start.3 = ((bf16[8,2,65536]{2,1,0:T(2,128)(2,1)}), bf16[8,2,65536]{2,1,0:T(2,128)(2,1)S(1)}, u32[]{:S(2)}, u32[]{:S(2)}) async-start(bf16[8,2,65536]{2,1,0:T(2,128)(2,1)} %reshape.230), calls=%async_computation.3 | async-start | bytes 4194304 | tf_op jit(solution)/shard_map/all_to_all | solution.py:73
  319.1 52.4 %all-to-all-start.1 = ((bf16[8,2,65536]{2,1,0:T(2,128)(2,1)}), bf16[8,2,65536]{2,1,0:T(2,128)(2,1)}, u32[]{:S(2)}, u32[]{:S(2)}) async-start(bf16[8,2,65536]{2,1,0:T(2,128)(2,1)} %reshape.228), calls=%async_computation.1 | async-start | bytes 4194304 | tf_op jit(solution)/shard_map/all_to_all | solution.py:72
Sparse Core Ops, SparseCore 0:
  20.3 40.1 all-gather.2
  62.6 57.2 all-gather.4
  224.2 69.8 reduce-scatter.1
where the time goes:
time: 409 us; the launch traced here: 401 us
  local copies, waits for them, and re-layouts  125 us (31%)
  waiting for transfers between devices  91 us (22%)
  other arithmetic  74.5 us (18%)
  matrix products  66.5 us (16%)
  starting transfers between devices  18.8 us (5%)
  between operations  16.1 us (4%)
  blocking collectives  8.89 us (2%)
    unnamed x28, local copies, waits for them, and re-layouts  88.7 us
    unnamed x4, other arithmetic  73.6 us
    all_to_all x1, waiting for transfers between devices, per_device(): lax.all_to_all(grad_out, 'ctx', split_axis=2, concat_axis=1, tiled=True)  36.9 us
    all_to_all x1, waiting for transfers between devices, per_device(): lax.all_to_all(head_out, 'ctx', split_axis=1, concat_axis=2, tiled=True)  34.2 us
    dot_general x1, matrix products, attend(): jnp.einsum('bhlj,bjhd->blhd', grad_scores, key, preferred_element_type=jn...  18.2 us
    dot_general x1, matrix products, attend(): jnp.einsum('bhlj,blhd->bjhd', grad_scores, q_rows, preferred_element_type...  14.9 us
    convert_element_type x1, local copies, waits for them, and re-layouts, attend(): attended = attended.reshape(batch, length, width).astype(jnp.bfloat16)  10.8 us
    all_to_all x1, waiting for transfers between devices, per_device(): lax.all_to_all(queries, 'ctx', split_axis=2, concat_axis=1, tiled=True)  9.97 us
  transfers between devices with their start and end apart: 7, of which 4 were waited for; matrix products, arithmetic and copies ran while one was open for 53% of the time, Pallas kernels for 0%

commit v1 on v0

v1 whole, which is shorter than its diff:
```python
import functools
import math

import jax
import jax.numpy as jnp
from jax import lax
from jax.experimental import pallas as pl
from jax.experimental.pallas import tpu as pltpu
from jax.sharding import PartitionSpec as P

HEAD = 128


def dot(a, b, dims):
    return lax.dot_general(a, b, (dims, ((), ())), preferred_element_type=jnp.float32)


def attend_kernel(heads, bias_ref, q_ref, g_ref, kv_ref, out_ref, gq_ref, gkv_ref):
    scale = 1.0 / math.sqrt(HEAD)
    bias = bias_ref[...]
    for h in range(heads):
        own = slice(h * HEAD, (h + 1) * HEAD)
        at_key = slice(2 * h * HEAD, (2 * h + 1) * HEAD)
        at_value = slice((2 * h + 1) * HEAD, (2 * h + 2) * HEAD)
        q = q_ref[:, own]
        g = g_ref[:, own]
        key = kv_ref[0, :, at_key]
        value = kv_ref[0, :, at_value]
        scores = dot(q, key, ((1,), (1,))) * scale + bias
        top = jnp.max(scores, axis=-1, keepdims=True)
        weights = jnp.exp(scores - top)
        probs = weights * (1.0 / jnp.sum(weights, axis=-1, keepdims=True))
        probs_low = probs.astype(jnp.bfloat16)
        out_ref[:, own] = dot(probs_low, value, ((1,), (0,))).astype(jnp.bfloat16)
        grad_probs = dot(g, value, ((1,), (1,)))
        delta = jnp.sum(probs * grad_probs, axis=-1, keepdims=True)
        grad_scores = (probs * (grad_probs - delta) * scale).astype(jnp.bfloat16)
        gq_ref[:, own] = dot(grad_scores, key, ((1,), (0,))).astype(jnp.bfloat16)
        gkv_ref[0, :, at_key] = dot(grad_scores, q, ((0,), (0,))).astype(gkv_ref.dtype)
        gkv_ref[0, :, at_value] = dot(probs_low, g, ((0,), (0,))).astype(gkv_ref.dtype)


def attend(bias, queries, grad_out, kv):
    length, width = queries.shape
    blocks, keys, columns = kv.shape
    per_block = columns // (2 * HEAD)
    heads = math.gcd(per_block, 4)
    steps = per_block // heads
    rows = pl.BlockSpec((length, heads * HEAD), lambda i, j: (0, i * steps + j))
    pairs = pl.BlockSpec((1, keys, heads * 2 * HEAD), lambda i, j: (i, 0, j))
    flops = 12 * length * keys * width
    return pl.pallas_call(
        functools.partial(attend_kernel, heads),
        grid=(blocks, steps),
        in_specs=[pl.BlockSpec((1, keys), lambda i, j: (0, 0)), rows, rows, pairs],
        out_specs=[rows, rows, pairs],
        out_shape=[
            jax.ShapeDtypeStruct(queries.shape, jnp.bfloat16),
            jax.ShapeDtypeStruct(queries.shape, jnp.bfloat16),
            jax.ShapeDtypeStruct(kv.shape, jnp.bfloat16),
        ],
        cost_estimate=pl.CostEstimate(
            flops=flops, bytes_accessed=2 * (4 * length * width + 2 * kv.size), transcendentals=length * keys * width // HEAD
        ),
        name="attend",
    )(bias, queries, grad_out, kv)


def greet(axis, a, last, up, down, partner):
    barrier = pltpu.get_barrier_semaphore()

    def hello(target):
        pl.semaphore_signal(barrier, inc=1, device_id={axis: target}, device_id_type=pl.DeviceIdType.MESH)

    hello(partner)

    @pl.when(a < last)
    def _():
        hello(up)

    @pl.when(a > 0)
    def _():
        hello(down)

    if last == 0:
        pl.semaphore_wait(barrier, 1)
    else:
        @pl.when((a > 0) & (a < last))
        def _():
            pl.semaphore_wait(barrier, 3)

        @pl.when((a == 0) | (a == last))
        def _():
            pl.semaphore_wait(barrier, 2)


def gather_kernel(axis, n, own_ref, out_ref, own_sem, send_sems, recv_sems):
    me = lax.axis_index(axis)
    a, b = me // 2, me % 2
    last = n // 2 - 1
    up, down, partner = me + 2, me - 2, a * 2 + (1 - b)
    greet(axis, a, last, up, down, partner)
    mine = pltpu.make_async_copy(own_ref, out_ref.at[me], own_sem)
    mine.start()

    def hop(source, block, way, target):
        return pltpu.make_async_remote_copy(
            src_ref=source, dst_ref=out_ref.at[block], send_sem=send_sems.at[block, way],
            recv_sem=recv_sems.at[block], device_id={axis: target}, device_id_type=pl.DeviceIdType.MESH,
        )

    @pl.when(a < last)
    def _():
        hop(own_ref, me, 0, up).start()

    @pl.when(a > 0)
    def _():
        hop(own_ref, me, 1, down).start()

    hop(own_ref, me, 2, partner).start()
    for s in range(1, last + 1):
        @pl.when(a >= s)
        def _():
            block = (a - s) * 2 + b
            hop(own_ref, block, 0, partner).wait_recv()

            @pl.when(a < last)
            def _():
                hop(out_ref.at[block], block, 0, up).start()

            hop(out_ref.at[block], block, 2, partner).start()

        @pl.when(a + s <= last)
        def _():
            block = (a + s) * 2 + b
            hop(own_ref, block, 1, partner).wait_recv()

            @pl.when(a > 0)
            def _():
                hop(out_ref.at[block], block, 1, down).start()

            hop(out_ref.at[block], block, 2, partner).start()

    for z in range(last + 1):
        hop(own_ref, z * 2 + 1 - b, 2, partner).wait_recv()
        hop(own_ref, z * 2 + b, 2, partner).wait_send()

        @pl.when((a < last) & (a >= z))
        def _():
            hop(own_ref, z * 2 + b, 0, partner).wait_send()

        @pl.when((a > 0) & (a <= z))
        def _():
            hop(own_ref, z * 2 + b, 1, partner).wait_send()

    mine.wait()


def gather(block, axis, n, collective_id):
    return pl.pallas_call(
        functools.partial(gather_kernel, axis, n),
        in_specs=[pl.BlockSpec(memory_space=pltpu.VMEM)],
        out_specs=pl.BlockSpec(memory_space=pl.ANY),
        out_shape=jax.ShapeDtypeStruct((n,) + block.shape, block.dtype),
        scratch_shapes=[
            pltpu.SemaphoreType.DMA,
            pltpu.SemaphoreType.DMA((n, 3)),
            pltpu.SemaphoreType.DMA((n,)),
        ],
        compiler_params=pltpu.CompilerParams(collective_id=collective_id, has_side_effects=True),
        name="gather",
    )(block)


def scatter_kernel(axis, n, g_ref, out_ref, crossed, risen, fallen, going, send_sems, x_sems, up_sems, down_sems):
    me = lax.axis_index(axis)
    a, b = me // 2, me % 2
    last = n // 2 - 1
    up, down, partner = me + 2, me - 2, a * 2 + (1 - b)
    greet(axis, a, last, up, down, partner)
    rows = out_ref.shape[0]
    step = min(rows, 32)
    half = (last + 2) // 2
    high = a // half

    def place(t):
        return high * t + (1 - high) * (last - t)

    def cross(z):
        return pltpu.make_async_remote_copy(
            src_ref=g_ref.at[z * 2 + 1 - b], dst_ref=crossed.at[z], send_sem=send_sems.at[z, 0],
            recv_sem=x_sems.at[z], device_id={axis: partner}, device_id_type=pl.DeviceIdType.MESH,
        )

    def rise(z):
        return pltpu.make_async_remote_copy(
            src_ref=going.at[z], dst_ref=risen.at[z], send_sem=send_sems.at[z, 1],
            recv_sem=up_sems.at[z], device_id={axis: up}, device_id_type=pl.DeviceIdType.MESH,
        )

    def fall(z):
        return pltpu.make_async_remote_copy(
            src_ref=going.at[z], dst_ref=fallen.at[z], send_sem=send_sems.at[z, 2],
            recv_sem=down_sems.at[z], device_id={axis: down}, device_id_type=pl.DeviceIdType.MESH,
        )

    def add(target, parts):
        @pl.loop(0, rows // step)
        def _(i):
            at = pl.ds(pl.multiple_of(i * step, step), step)
            total = parts[0][at, :].astype(jnp.float32)
            for part in parts[1:]:
                total = total + part[at, :].astype(jnp.float32)
            target[at, :] = total.astype(target.dtype)

    for t in range(last + 1):
        cross(place(t)).start()
    for t in range(last + 1):
        z = place(t)
        cross(z).wait_recv()
        pair = [g_ref.at[z * 2 + b], crossed.at[z]]

        @pl.when(z > a)
        def _():
            @pl.when(a > 0)
            def _():
                rise(z).wait_recv()
                add(going.at[z], pair + [risen.at[z]])

            @pl.when(a == 0)
            def _():
                add(going.at[z], pair)

            rise(z).start()

        @pl.when(z < a)
        def _():
            @pl.when(a < last)
            def _():
                fall(z).wait_recv()
                add(going.at[z], pair + [fallen.at[z]])

            @pl.when(a == last)
            def _():
                add(going.at[z], pair)

            fall(z).start()

    pair = [g_ref.at[a * 2 + b], crossed.at[a]]

    @pl.when(a > 0)
    def _():
        rise(a).wait_recv()

    @pl.when(a < last)
    def _():
        fall(a).wait_recv()

    @pl.when(a == 0)
    def _():
        add(out_ref, pair + [fallen.at[a]])

    @pl.when(a == last)
    def _():
        add(out_ref, pair + [risen.at[a]])

    @pl.when((a > 0) & (a < last))
    def _():
        add(out_ref, pair + [risen.at[a], fallen.at[a]])

    for z in range(last + 1):
        cross(z).wait_send()

        @pl.when(z > a)
        def _():
            rise(z).wait_send()

        @pl.when(z < a)
        def _():
            fall(z).wait_send()


def scatter(parts, axis, collective_id):
    n, rows, columns = parts.shape
    half = n // 2
    blocks = pltpu.VMEM((half, rows, columns), parts.dtype)
    return pl.pallas_call(
        functools.partial(scatter_kernel, axis, n),
        in_specs=[pl.BlockSpec(memory_space=pltpu.VMEM)],
        out_specs=pl.BlockSpec(memory_space=pltpu.VMEM),
        out_shape=jax.ShapeDtypeStruct((rows, columns), jnp.bfloat16),
        scratch_shapes=[blocks] * 4
        + [
            pltpu.SemaphoreType.DMA((half, 3)),
            pltpu.SemaphoreType.DMA((half,)),
            pltpu.SemaphoreType.DMA((half,)),
            pltpu.SemaphoreType.DMA((half,)),
        ],
        compiler_params=pltpu.CompilerParams(
            collective_id=collective_id, has_side_effects=True, vmem_limit_bytes=40 << 20
        ),
        name="scatter",
    )(parts)


def per_device(groups, text, src, lengths, kv_weight, queries, grad_out):
    dp, ctx = groups
    group = lax.axis_index("dp")
    samples = src.shape[0]
    share = ctx // dp
    tokens = text.shape[2]
    keys = 2 * tokens
    features = kv_weight.shape[0]
    columns = kv_weight.shape[2]
    hops = [
        (d * ctx + c, (c // share) * ctx + d * share + c % share)
        for d in range(dp)
        for c in range(ctx)
    ]
    mine = lax.ppermute(text[0], ("dp", "ctx"), hops)
    pieces = gather(mine.reshape(2 * tokens, -1), "ctx", ctx, 1)
    pieces = pieces.reshape(samples, share, 2, tokens, features // share)
    by_text = jnp.transpose(pieces, (0, 2, 3, 1, 4)).reshape(samples, 2, tokens, features)
    rows = jnp.stack(
        [lax.dynamic_index_in_dim(by_text, src[b], 0, keepdims=False) for b in range(samples)]
    )
    partial = jnp.einsum("betf,fec->betc", rows, kv_weight, preferred_element_type=jnp.float32)
    kv_local = scatter(partial.reshape(samples, keys, columns), "dp", 4)
    kv = gather(kv_local, "ctx", ctx, 2)
    own_lengths = lax.dynamic_index_in_dim(lengths, src[group], 0, keepdims=False)
    valid = jnp.arange(tokens, dtype=jnp.int32)[None, :] < own_lengths[:, None]
    bias = jnp.where(valid, 0.0, -1e30).astype(jnp.float32).reshape(1, keys)
    attended, grad_queries, grad_kv = attend(bias, queries[0], grad_out[0], kv)
    grad_low = scatter(grad_kv, "ctx", 3)
    grads = gather(grad_low, "dp", dp, 5)
    grads = grads.reshape(samples, 2, tokens, columns)
    grad_weight = jnp.einsum("betf,betc->fec", rows, grads, preferred_element_type=jnp.float32)
    return (attended[None], grad_queries[None], grad_weight)


def solution(mesh):
    placed = (
        P("dp", None, None, "ctx"),
        P(),
        P(),
        P("dp", None, "ctx"),
        P("dp", "ctx", None),
        P("dp", "ctx", None),
    )
    return jax.shard_map(
        functools.partial(per_device, (mesh.shape["dp"], mesh.shape["ctx"])),
        mesh=mesh,
        in_specs=placed,
        out_specs=(P("dp", "ctx", None), P("dp", "ctx", None), P("dp", None, "ctx")),
        check_vma=False,
    )
```

time: 409 us -> 242 us (0.59); the launches traced: 401 us -> 242 us
  Pallas kernels: 0 us -> 202 us
  local copies, waits for them, and re-layouts: 125 us -> 20.3 us
  waiting for transfers between devices: 91 us -> 0.01 us
  other arithmetic: 74.5 us -> 0.67 us
  matrix products: 66.5 us -> 6.23 us
  starting transfers between devices: 18.8 us -> 1.69 us
  blocking collectives: 8.89 us -> 0 us
  between operations: 16.1 us -> 10.2 us
    pallas_call x0 -> x6, Pallas kernels: none -> 202 us  [the longest x3 92.9 us: gather(): pl.pallas_call(functools.partial(gather_kernel, axis, n), in_specs=[pl.Bl...]
    all_to_all x4 -> x0, waiting for transfers between devices: 90.9 us -> none  [the longest x1 36.9 us: per_device(): lax.all_to_all(grad_out, 'ctx', split_axis=2, concat_axis=1, tiled=True)]
    unnamed x28 -> x23, local copies, waits for them, and re-layouts: 88.7 us -> 12.6 us
    unnamed x4 -> x0, other arithmetic: 73.6 us -> none
    dot_general x7 -> x2, matrix products: 58.5 us -> 6.23 us  [the longest x1 4.84 us: per_device(): jnp.einsum('betf,betc->fec', rows, grads, preferred_element_type=jnp.floa...]
    convert_element_type x3 -> x0, local copies, waits for them, and re-layouts: 18.6 us -> none  [the longest x1 10.8 us: attend(): attended = attended.reshape(batch, length, width).astype(jnp.bfloat16)]
    all_to_all x4 -> x0, starting transfers between devices: 18.3 us -> none  [the longest x1 5.81 us: per_device(): lax.all_to_all(queries, 'ctx', split_axis=2, concat_axis=1, tiled=True)]
    all_gather x1 -> x0, blocking collectives: 8.89 us -> none  [per_device(): everyone = lax.all_gather(text, 'dp', axis=0, tiled=True)]
  transfers between devices with their start and end apart: 7 -> 1, of which waited for: 4 -> 0; matrix products, arithmetic and copies ran while one was open for 53% -> 1% of each run, Pallas kernels for 0% -> 0%
where the time goes in v1:
time: 242 us
  Pallas kernels  202 us (83%)
  local copies, waits for them, and re-layouts  20.3 us (8%)
  between operations  10.2 us (4%)
  matrix products  6.23 us (3%)
    pallas_call x3, Pallas kernels, gather(): pl.pallas_call(functools.partial(gather_kernel, axis, n), in_specs=[pl.Bl...  92.9 us
    pallas_call x2, Pallas kernels, scatter(): pl.pallas_call(functools.partial(scatter_kernel, axis, n), in_specs=[pl.B...  86.1 us
    pallas_call x1, Pallas kernels, attend(): pl.pallas_call(functools.partial(attend_kernel, heads), grid=(blocks, ste...  23.4 us
    unnamed x23, local copies, waits for them, and re-layouts  12.6 us
    dot_general x1, matrix products, per_device(): jnp.einsum('betf,betc->fec', rows, grads, preferred_element_type=jnp.floa...  4.84 us
  transfers between devices with their start and end apart: 1, of which 0 were waited for; matrix products, arithmetic and copies ran while one was open for 1% of the time, Pallas kernels for 0%

profile of v1, /device:TPU:0, one launch (start us, length us, event | category | flops | bytes accessed | tf_op | source)
XLA Modules:
  0.0 241.6 jit_solution(16067946392940666447)
XLA Ops:
  0.6 0.0 copy-start
  0.6 1.7 collective-permute-start
  2.3 1.5 fusion.3
  13.2 0.9 fusion.2
  14.1 0.7 compare_select_fusion
  14.7 0.0 collective-permute-done
  14.7 0.0 copy-start.10
  14.7 0.7 copy-done.10
  15.4 24.6 %gather.3 = bf16[8,256,256]{2,1,0:T(8,128)(2,1)} custom-call(bf16[256,256]{1,0:T(8,128)(2,1)} %bitcast.31), custom_call_target="tpu_custom_call" | custom-call | tf_op jit(solution)/shard_map/gather/pallas_call | solution.py:160
  40.0 3.3 %copy.9 = bf16[4,2,128,2,256]{4,3,2,0,1:T(2,128)(2,1)} copy(bf16[4,2,128,2,256]{4,2,1,3,0:T(8,128)(2,1)} %bitcast.29) | data formatting | bytes 2097152 | tf_op jit(solution)/shard_map/transpose | solution.py:323
  43.3 1.7 reshape.54
  45.0 0.1 constant_dynamic-slice_fusion.3
  45.1 0.0 copy-done
  45.1 0.0 copy-start.4
  45.1 0.0 copy-start.6
  45.1 0.0 copy-start.8
  45.1 0.7 copy-done.4
  45.8 0.1 copy-done.6
  45.9 0.1 copy-done.8
  46.0 1.4 convolution_bitcast_fusion.1
  47.4 0.3 copy.11
  47.7 29.7 %scatter.2.own_ref = bf16[256,1024]{1,0:T(8,128)(2,1)S(1)} custom-call(f32[4,256,1024]{2,1,0:T(8,128)S(1)} %bitcast.28), custom_call_target="tpu_custom_call" | custom-call | tf_op jit(solution)/shard_map/scatter/pallas_call | solution.py:287
  77.4 0.0 copy-start.2
  77.4 0.8 copy-done.2
  78.2 49.4 %gather.4.kv_ref = bf16[8,256,1024]{2,1,0:T(8,128)(2,1)} custom-call(bf16[256,1024]{1,0:T(8,128)(2,1)} %copy-done.2), custom_call_target="tpu_custom_call" | custom-call | tf_op jit(solution)/shard_map/gather/pallas_call | solution.py:160
  127.6 23.4 %attend.1 = (bf16[256,4096]{1,0:T(8,128)(2,1)}, bf16[256,4096]{1,0:T(8,128)(2,1)}, bf16[8,256,1024]{2,1,0:T(8,128)(2,1)}) custom-call(f32[1,256]{1,0:T(1,128)} %bitcast.37, bf16[256,4096]{1,0:T(8,128)(2,1)} %bitcast.32, bf16[256,4096]{1,0:T(8,128)(2,1)} %bitcast.33, bf16[8,256,1024]{2,1,0:T(8,128)(2,1)} %gather.4.kv_ref), custom_call_target="tpu_custom_call" | custom-call | flops 3221225472 | bytes 16777216 | tf_op jit(solution)/shard_map/attend/pallas_call | solution.py:52
  151.1 0.0 copy-start.1
  151.1 2.2 copy-done.1
  153.2 56.4 %scatter.3.own_ref = bf16[256,1024]{1,0:T(8,128)(2,1)S(1)} custom-call(bf16[8,256,1024]{2,1,0:T(8,128)(2,1)S(1)} %copy-done.1), custom_call_target="tpu_custom_call" | custom-call | tf_op jit(solution)/shard_map/scatter/pallas_call | solution.py:287
  209.6 0.0 copy-start.3
  209.6 0.8 copy-done.3
  210.4 0.0 copy-start.5
  210.4 0.0 copy-start.7
  210.4 0.0 copy-start.9
  210.4 19.0 %gather.5 = bf16[4,256,1024]{2,1,0:T(8,128)(2,1)} custom-call(bf16[256,1024]{1,0:T(8,128)(2,1)} %copy-done.3), custom_call_target="tpu_custom_call" | custom-call | tf_op jit(solution)/shard_map/gather/pallas_call | solution.py:160
  229.4 0.0 copy-done.5
  229.4 0.0 copy-done.7
  229.4 0.0 copy-done.9
  229.4 4.8 %convolution_bitcast_fusion = f32[512,2,1024]{0,2,1:T(8,128)} fusion(bf16[4,2,128,1024]{3,2,1,0:T(8,128)(2,1)} %bitcast.30, bf16[1,2,128,512]{3,2,0,1:T(8,128)(2,1)S(1)} %copy-done.5, bf16[1,2,128,512]{3,2,0,1:T(8,128)(2,1)S(1)} %copy-done.7, bf16[1,2,128,512]{3,2,0,1:T(8,128)(2,1)S(1)} %copy-done.9, bf16[1,2,128,512]{3,2,0,1:T(8,128)(2,1)S(1)} %get-tuple-element.12), kind=kOutput, calls=%fused_computation | convolution fusion | flops 1075314688 | bytes 7340032 | tf_op jit(solution)/shard_map/betf,betc->fec/dot_general | solution.py:337
  234.3 7.3 %copy.13 = f32[512,2,1024]{2,1,0:T(2,128)} copy(f32[512,2,1024]{0,2,1:T(8,128)} %convolution_bitcast_fusion) | data formatting | bytes 8388608
Async XLA Ops:
  0.6 44.5 %copy-start = (bf16[512,2,1024]{2,1,0:T(2,128)(2,1)S(1)}, bf16[512,2,1024]{2,1,0:T(2,128)(2,1)}, u32[]{:S(2)}) copy-start(bf16[512,2,1024]{2,1,0:T(2,128)(2,1)} %param.9) | copy-start | bytes 6291460
  0.6 14.1 %collective-permute-start = (bf16[2,128,256]{2,1,0:T(8,128)(2,1)}, bf16[2,128,256]{2,1,0:T(8,128)(2,1)S(1)}, u32[]{:S(2)}, u32[]{:S(2)}) collective-permute-start(bf16[2,128,256]{2,1,0:T(8,128)(2,1)} %bitcast.34), channel_id=1, source_target_pairs={{0,0},{1,1},{2,8},{3,9},{4,16},{5,17},{6,24},{7,25},{8,2},{9,3},{1... | collective-permute-start | bytes 393224 | tf_op jit(solution)/shard_map/ppermute | solution.py:320
  14.7 0.7 copy-start.10
  45.1 0.7 copy-start.4
  45.1 0.8 copy-start.6
  45.1 0.9 copy-start.8
  77.4 0.8 copy-start.2
  151.1 2.2 copy-start.1
  209.6 0.8 copy-start.3
  210.4 19.0 %copy-start.5 = (bf16[1,2,128,512]{3,2,0,1:T(8,128)(2,1)S(1)}, bf16[1,2,128,512]{3,2,0,1:T(8,128)(2,1)}, u32[]{:S(2)}) copy-start(bf16[1,2,128,512]{3,2,0,1:T(8,128)(2,1)} %copy-done.4) | copy-start | bytes 786436
  210.4 19.0 %copy-start.7 = (bf16[1,2,128,512]{3,2,0,1:T(8,128)(2,1)S(1)}, bf16[1,2,128,512]{3,2,0,1:T(8,128)(2,1)}, u32[]{:S(2)}) copy-start(bf16[1,2,128,512]{3,2,0,1:T(8,128)(2,1)} %copy-done.6) | copy-start | bytes 786436
  210.4 19.0 %copy-start.9 = (bf16[1,2,128,512]{3,2,0,1:T(8,128)(2,1)S(1)}, bf16[1,2,128,512]{3,2,0,1:T(8,128)(2,1)}, u32[]{:S(2)}) copy-start(bf16[1,2,128,512]{3,2,0,1:T(8,128)(2,1)} %copy-done.8) | copy-start | bytes 786436

commit v2 on v1

--- a/solution.py
+++ b/solution.py
@@ -15,17 +15,18 @@
     return lax.dot_general(a, b, (dims, ((), ())), preferred_element_type=jnp.float32)
 
 
-def attend_kernel(heads, bias_ref, q_ref, g_ref, kv_ref, out_ref, gq_ref, gkv_ref):
+def attend_block(block, bias_ref, q_ref, g_ref, kv_ref, out_ref, gq_ref, gkv_ref):
     scale = 1.0 / math.sqrt(HEAD)
     bias = bias_ref[...]
+    heads = kv_ref.shape[2] // (2 * HEAD)
     for h in range(heads):
-        own = slice(h * HEAD, (h + 1) * HEAD)
+        own = pl.ds(pl.multiple_of((block * heads + h) * HEAD, HEAD), HEAD)
         at_key = slice(2 * h * HEAD, (2 * h + 1) * HEAD)
         at_value = slice((2 * h + 1) * HEAD, (2 * h + 2) * HEAD)
         q = q_ref[:, own]
         g = g_ref[:, own]
-        key = kv_ref[0, :, at_key]
-        value = kv_ref[0, :, at_value]
+        key = kv_ref[block, :, at_key]
+        value = kv_ref[block, :, at_value]
         scores = dot(q, key, ((1,), (1,))) * scale + bias
         top = jnp.max(scores, axis=-1, keepdims=True)
         weights = jnp.exp(scores - top)
@@ -36,34 +37,8 @@
         delta = jnp.sum(probs * grad_probs, axis=-1, keepdims=True)
         grad_scores = (probs * (grad_probs - delta) * scale).astype(jnp.bfloat16)
         gq_ref[:, own] = dot(grad_scores, key, ((1,), (0,))).astype(jnp.bfloat16)
-        gkv_ref[0, :, at_key] = dot(grad_scores, q, ((0,), (0,))).astype(gkv_ref.dtype)
-        gkv_ref[0, :, at_value] = dot(probs_low, g, ((0,), (0,))).astype(gkv_ref.dtype)
-
-
-def attend(bias, queries, grad_out, kv):
-    length, width = queries.shape
-    blocks, keys, columns = kv.shape
-    per_block = columns // (2 * HEAD)
-    heads = math.gcd(per_block, 4)
-    steps = per_block // heads
-    rows = pl.BlockSpec((length, heads * HEAD), lambda i, j: (0, i * steps + j))
-    pairs = pl.BlockSpec((1, keys, heads * 2 * HEAD), lambda i, j: (i, 0, j))
-    flops = 12 * length * keys * width
-    return pl.pallas_call(
-        functools.partial(attend_kernel, heads),
-        grid=(blocks, steps),
-        in_specs=[pl.BlockSpec((1, keys), lambda i, j: (0, 0)), rows, rows, pairs],
-        out_specs=[rows, rows, pairs],
-        out_shape=[
-            jax.ShapeDtypeStruct(queries.shape, jnp.bfloat16),
-            jax.ShapeDtypeStruct(queries.shape, jnp.bfloat16),
-            jax.ShapeDtypeStruct(kv.shape, jnp.bfloat16),
-        ],
-        cost_estimate=pl.CostEstimate(
-            flops=flops, bytes_accessed=2 * (4 * length * width + 2 * kv.size), transcendentals=length * keys * width // HEAD
-        ),
-        name="attend",
-    )(bias, queries, grad_out, kv)
+        gkv_ref[block, :, at_key] = dot(grad_scores, q, ((0,), (0,))).astype(gkv_ref.dtype)
+        gkv_ref[block, :, at_value] = dot(probs_low, g, ((0,), (0,))).astype(gkv_ref.dtype)
 
 
 def greet(axis, a, last, up, down, partner):
@@ -172,7 +147,7 @@
     )(block)
 
 
-def scatter_kernel(axis, n, g_ref, out_ref, crossed, risen, fallen, going, send_sems, x_sems, up_sems, down_sems):
+def scatter_kernel(axis, n, compute, g_ref, out_ref, crossed, risen, fallen, going, send_sems, x_sems, up_sems, down_sems):
     me = lax.axis_index(axis)
     a, b = me // 2, me % 2
     last = n // 2 - 1
@@ -213,8 +188,19 @@
                 total = total + part[at, :].astype(jnp.float32)
             target[at, :] = total.astype(target.dtype)
 
-    for t in range(last + 1):
-        cross(place(t)).start()
+    if compute is None:
+        for t in range(last + 1):
+            cross(place(t)).start()
+    else:
+        @pl.loop(0, last + 1)
+        def _(t):
+            compute(place(t) * 2 + 1 - b)
+            cross(place(t)).start()
+
+        @pl.loop(0, last + 1)
+        def _(t):
+            compute(place(t) * 2 + b)
+
     for t in range(last + 1):
         z = place(t)
         cross(z).wait_recv()
@@ -285,7 +271,7 @@
     half = n // 2
     blocks = pltpu.VMEM((half, rows, columns), parts.dtype)
     return pl.pallas_call(
-        functools.partial(scatter_kernel, axis, n),
+        functools.partial(scatter_kernel, axis, n, None),
         in_specs=[pl.BlockSpec(memory_space=pltpu.VMEM)],
         out_specs=pl.BlockSpec(memory_space=pltpu.VMEM),
         out_shape=jax.ShapeDtypeStruct((rows, columns), jnp.bfloat16),
@@ -301,6 +287,42 @@
         ),
         name="scatter",
     )(parts)
+
+
+def attend_kernel(axis, n, bias_ref, q_ref, g_ref, kv_ref, out_ref, gq_ref, sum_ref, gkv_ref, *rest):
+    def compute(block):
+        attend_block(block, bias_ref, q_ref, g_ref, kv_ref, out_ref, gq_ref, gkv_ref)
+
+    scatter_kernel(axis, n, compute, gkv_ref, sum_ref, *rest)
+
+
+def attend(bias, queries, grad_out, kv, axis, collective_id):
+    n, rows, columns = kv.shape
+    half = n // 2
+    blocks = pltpu.VMEM((half, rows, columns), jnp.bfloat16)
+    vmem = pl.BlockSpec(memory_space=pltpu.VMEM)
+    return pl.pallas_call(
+        functools.partial(attend_kernel, axis, n),
+        in_specs=[vmem] * 4,
+        out_specs=[vmem] * 3,
+        out_shape=[
+            jax.ShapeDtypeStruct(queries.shape, jnp.bfloat16),
+            jax.ShapeDtypeStruct(queries.shape, jnp.bfloat16),
+            jax.ShapeDtypeStruct((rows, columns), jnp.bfloat16),
+        ],
+        scratch_shapes=[pltpu.VMEM(kv.shape, jnp.bfloat16)]
+        + [blocks] * 4
+        + [
+            pltpu.SemaphoreType.DMA((half, 3)),
+            pltpu.SemaphoreType.DMA((half,)),
+            pltpu.SemaphoreType.DMA((half,)),
+            pltpu.SemaphoreType.DMA((half,)),
+        ],
+        compiler_params=pltpu.CompilerParams(
+            collective_id=collective_id, has_side_effects=True, vmem_limit_bytes=48 << 20
+        ),
+        name="attend",
+    )(bias, queries, grad_out, kv)
 
 
 def per_device(groups, text, src, lengths, kv_weight, queries, grad_out):
@@ -330,8 +352,7 @@
     own_lengths = lax.dynamic_index_in_dim(lengths, src[group], 0, keepdims=False)
     valid = jnp.arange(tokens, dtype=jnp.int32)[None, :] < own_lengths[:, None]
     bias = jnp.where(valid, 0.0, -1e30).astype(jnp.float32).reshape(1, keys)
-    attended, grad_queries, grad_kv = attend(bias, queries[0], grad_out[0], kv)
-    grad_low = scatter(grad_kv, "ctx", 3)
+    attended, grad_queries, grad_low = attend(bias, queries[0], grad_out[0], kv, "ctx", 3)
     grads = gather(grad_low, "dp", dp, 5)
     grads = grads.reshape(samples, 2, tokens, columns)
     grad_weight = jnp.einsum("betf,betc->fec", rows, grads, preferred_element_type=jnp.float32)

time: 242 us -> 230 us (0.950)
  Pallas kernels: 202 us -> 185 us
  local copies, waits for them, and re-layouts: 20.3 us -> 25.4 us
    pallas_call x3 -> x2, Pallas kernels: 109 us -> 92.2 us  [the longest x1 62.5 us: attend(): pl.pallas_call(functools.partial(attend_kernel, axis, n), in_specs=[vmem]...]
    unnamed x23 -> x29, local copies, waits for them, and re-layouts: 12.6 us -> 17.7 us
where the time goes in v2:
time: 230 us; the launch traced here: 229 us
  Pallas kernels  185 us (80%)
  local copies, waits for them, and re-layouts  25.4 us (11%)
  between operations  10.4 us (5%)
  matrix products  6.24 us (3%)
    pallas_call x3, Pallas kernels, gather(): pl.pallas_call(functools.partial(gather_kernel, axis, n), in_specs=[pl.Bl...  92.9 us
    pallas_call x1, Pallas kernels, attend(): pl.pallas_call(functools.partial(attend_kernel, axis, n), in_specs=[vmem]...  62.5 us
    pallas_call x1, Pallas kernels, scatter(): pl.pallas_call(functools.partial(scatter_kernel, axis, n, None), in_specs...  29.7 us
    unnamed x29, local copies, waits for them, and re-layouts  17.7 us
    dot_general x1, matrix products, per_device(): jnp.einsum('betf,betc->fec', rows, grads, preferred_element_type=jnp.floa...  4.85 us
  transfers between devices with their start and end apart: 1, of which 0 were waited for; matrix products, arithmetic and copies ran while one was open for 1% of the time, Pallas kernels for 0%

profile of v2, /device:TPU:0, one launch (start us, length us, event | category | flops | bytes accessed | tf_op | source)
XLA Modules:
  0.0 228.9 jit_solution(6128898298032050952)
XLA Ops:
  0.6 0.0 copy-start
  0.6 1.7 collective-permute-start
  2.3 1.5 fusion.3
  13.4 0.9 fusion.2
  14.3 0.1 compare_select_fusion
  14.4 0.0 collective-permute-done
  14.4 0.0 copy-start.12
  14.4 0.7 copy-done.12
  15.0 24.6 %gather.3 = bf16[8,256,256]{2,1,0:T(8,128)(2,1)} custom-call(bf16[256,256]{1,0:T(8,128)(2,1)} %bitcast.36), custom_call_target="tpu_custom_call" | custom-call | tf_op jit(solution)/shard_map/gather/pallas_call | solution.py:135
  39.6 3.3 %copy.9 = bf16[4,2,128,2,256]{4,3,2,0,1:T(2,128)(2,1)} copy(bf16[4,2,128,2,256]{4,2,1,3,0:T(8,128)(2,1)} %bitcast.32) | data formatting | bytes 2097152 | tf_op jit(solution)/shard_map/transpose | solution.py:345
  42.9 1.7 reshape.54
  44.6 0.1 constant_dynamic-slice_fusion.3
  44.7 0.0 copy-done
  44.7 0.0 copy-start.6
  44.7 0.0 copy-start.8
  44.7 0.0 copy-start.10
  44.7 0.7 copy-done.6
  45.4 0.1 copy-done.8
  45.5 0.1 copy-done.10
  45.6 1.4 convolution_bitcast_fusion.1
  47.0 0.3 copy.11
  47.3 29.7 %scatter.1.own_ref = bf16[256,1024]{1,0:T(8,128)(2,1)S(1)} custom-call(f32[4,256,1024]{2,1,0:T(8,128)S(1)} %bitcast.28), custom_call_target="tpu_custom_call" | custom-call | tf_op jit(solution)/shard_map/scatter/pallas_call | solution.py:273
  77.0 0.0 copy-start.1
  77.1 0.8 copy-done.1
  77.8 49.4 %gather.4.kv_ref = bf16[8,256,1024]{2,1,0:T(8,128)(2,1)} custom-call(bf16[256,1024]{1,0:T(8,128)(2,1)} %copy-done.1), custom_call_target="tpu_custom_call" | custom-call | tf_op jit(solution)/shard_map/gather/pallas_call | solution.py:135
  127.2 62.5 %attend.1 = (bf16[256,4096]{1,0:T(8,128)(2,1)S(1)}, bf16[256,4096]{1,0:T(8,128)(2,1)S(1)}, bf16[256,1024]{1,0:T(8,128)(2,1)S(1)}) custom-call(f32[1,256]{1,0:T(1,128)S(1)} %bitcast.31, bf16[256,4096]{1,0:T(8,128)(2,1)} %bitcast.33, bf16[256,4096]{1,0:T(8,128)(2,1)} %bitcast.34, bf16[8,256,1024]{2,1,0:T(8,128)(2,1)} %gather.4.kv_ref), custom_call_target="tpu_custom_call" | custom-call | tf_op jit(solution)/shard_map/attend/pallas_call | solution.py:304
  189.7 0.0 copy-start.2
  189.8 1.3 copy-done.2
  191.1 0.0 copy-start.4
  191.1 1.3 copy-done.4
  192.4 0.0 copy-start.5
  192.4 0.8 copy-done.5
  193.2 0.0 copy-start.7
  193.2 0.0 copy-start.9
  193.2 0.0 copy-start.11
  193.2 19.0 %gather.5 = bf16[4,256,1024]{2,1,0:T(8,128)(2,1)} custom-call(bf16[256,1024]{1,0:T(8,128)(2,1)} %copy-done.5), custom_call_target="tpu_custom_call" | custom-call | tf_op jit(solution)/shard_map/gather/pallas_call | solution.py:135
  212.2 0.0 copy-done.7
  212.2 0.0 copy-done.9
  212.2 0.0 copy-done.11
  212.2 4.8 %convolution_bitcast_fusion = f32[512,2,1024]{0,2,1:T(8,128)} fusion(bf16[4,2,128,1024]{3,2,1,0:T(8,128)(2,1)} %bitcast.35, bf16[1,2,128,512]{3,2,0,1:T(8,128)(2,1)S(1)} %copy-done.7, bf16[1,2,128,512]{3,2,0,1:T(8,128)(2,1)S(1)} %copy-done.9, bf16[1,2,128,512]{3,2,0,1:T(8,128)(2,1)S(1)} %copy-done.11, bf16[1,2,128,512]{3,2,0,1:T(8,128)(2,1)S(1)} %get-tuple-element.12), kind=kOutput, calls=%fused_computation | convolution fusion | flops 1075314688 | bytes 7340032 | tf_op jit(solution)/shard_map/betf,betc->fec/dot_general | solution.py:358
  217.0 7.3 %copy.13 = f32[512,2,1024]{2,1,0:T(2,128)} copy(f32[512,2,1024]{0,2,1:T(8,128)} %convolution_bitcast_fusion) | data formatting | bytes 8388608
  224.3 0.0 copy-start.3
  224.3 3.3 %copy.25 = bf16[1,256,4096]{2,1,0:T(8,128)(2,1)} copy(bf16[1,256,4096]{2,1,0:T(8,128)(2,1)} %bitcast.30) | data formatting | bytes 4194304
  227.6 0.0 copy-done.3
  227.6 1.3 copy.26
Async XLA Ops:
  0.6 44.1 %copy-start = (bf16[512,2,1024]{2,1,0:T(2,128)(2,1)S(1)}, bf16[512,2,1024]{2,1,0:T(2,128)(2,1)}, u32[]{:S(2)}) copy-start(bf16[512,2,1024]{2,1,0:T(2,128)(2,1)} %param.9) | copy-start | bytes 6291460
  0.6 13.7 %collective-permute-start = (bf16[2,128,256]{2,1,0:T(8,128)(2,1)}, bf16[2,128,256]{2,1,0:T(8,128)(2,1)S(1)}, u32[]{:S(2)}, u32[]{:S(2)}) collective-permute-start(bf16[2,128,256]{2,1,0:T(8,128)(2,1)} %bitcast.37), channel_id=1, source_target_pairs={{0,0},{1,1},{2,8},{3,9},{4,16},{5,17},{6,24},{7,25},{8,2},{9,3},{1... | collective-permute-start | bytes 393224 | tf_op jit(solution)/shard_map/ppermute | solution.py:342
  14.4 0.7 copy-start.12
  44.7 0.7 copy-start.6
  44.7 0.8 copy-start.8
  44.7 0.9 copy-start.10
  77.0 0.8 copy-start.1
  189.7 1.3 copy-start.2
  191.1 1.3 copy-start.4
  192.4 0.8 copy-start.5
  193.2 19.0 %copy-start.7 = (bf16[1,2,128,512]{3,2,0,1:T(8,128)(2,1)S(1)}, bf16[1,2,128,512]{3,2,0,1:T(8,128)(2,1)}, u32[]{:S(2)}) copy-start(bf16[1,2,128,512]{3,2,0,1:T(8,128)(2,1)} %copy-done.6) | copy-start | bytes 786436
  193.2 19.0 %copy-start.9 = (bf16[1,2,128,512]{3,2,0,1:T(8,128)(2,1)S(1)}, bf16[1,2,128,512]{3,2,0,1:T(8,128)(2,1)}, u32[]{:S(2)}) copy-start(bf16[1,2,128,512]{3,2,0,1:T(8,128)(2,1)} %copy-done.8) | copy-start | bytes 786436
  193.2 19.0 %copy-start.11 = (bf16[1,2,128,512]{3,2,0,1:T(8,128)(2,1)S(1)}, bf16[1,2,128,512]{3,2,0,1:T(8,128)(2,1)}, u32[]{:S(2)}) copy-start(bf16[1,2,128,512]{3,2,0,1:T(8,128)(2,1)} %copy-done.10) | copy-start | bytes 786436
  224.3 3.3 %copy-start.3 = (bf16[256,4096]{1,0:T(8,128)(2,1)S(1)}, bf16[256,4096]{1,0:T(8,128)(2,1)}, u32[]{:S(2)}) copy-start(bf16[256,4096]{1,0:T(8,128)(2,1)} %copy-done.2) | copy-start | bytes 6291460
